TPU v7x, 32 devices: a whole 2x2x4 slice. The times are simulated.
32 devices in a mesh: groups: 2 (over y), tensor: 4 (over z), dp: 2 (over x), kv: 2 (over core).
Axes of the slice: x: 2, y: 2, z: 4, core: 2. Of those that a mesh axis runs over, the one named last changes fastest.
Arguments:
- residual: bfloat16 [64, 16384], P(('groups', 'dp'), ('tensor', 'kv')), parts along dimension 0, may hold values from -10 to 10
- query: bfloat16 [64, 8192], P(('groups', 'dp'), ('tensor', 'kv')), parts along dimension 0, may hold values from -60 to 60
- new_pair: bfloat16 [2, 64, 4, 128], P(None, ('groups', 'dp')), parts along dimension 1, may hold values from -8 to 8
- kv_cache: bfloat16 [2, 64, 2048, 4, 128], P(None, ('groups', 'dp'), ('tensor', 'kv')), parts along dimension 1, may hold values from -4.5 to 4.5
- lengths: int32 [64], P(('groups', 'dp')), parts along dimension 0, may hold values from 2 to 2048
- out_weight: bfloat16 [8192, 16384], P(('tensor', 'kv')), may hold values from -0.09375 to 0.09375
- norm_gain: bfloat16 [16384], replicated, may hold values from 0.25 to 1.75
Outputs:
- residual_out: bfloat16 [64, 16384], P(('groups', 'dp'), ('tensor', 'kv')), parts along dimension 0
- mlp_input: bfloat16 [64, 16384], P(('groups', 'dp')), parts along dimension 0
There are 2 independent parts, one for each index of `groups`. A program takes and returns all parts, laid end to end along the dimension named above; an argument that names none is the same for every part. Nothing has to cross between parts.
Inputs may be any that keep to these rules, and one draw needn't show every extreme that they name: Positions below lengths[b] hold sequence b's cache; the others are ignored.
All inputs are finite; a program needn't handle non-finite values.
Results may differ from a plain program's by a relative error of at most 0.007.
Values may be sent and summed in bfloat16 or wider, within the bound.
A program may use at most 128 MiB of HBM per device.

v0:
```python
import math
import jax
import jax.numpy as jnp
from jax import lax
from jax.sharding import PartitionSpec as P

D = 16384
QH = 64
KVH = 4
HD = 128
floor_value = -1e30
epsilon = 1e-05


def on_device(residual, query, new_pair, kv_cache, lengths, out_weight, norm_gain):
    seqs = residual.shape[0]
    width = residual.shape[1]
    per_dev = query.shape[1] // HD
    group = QH // KVH
    scaling = 1.0 / math.sqrt(HD)
    mine = lax.axis_index(("tensor", "kv"))
    queries = lax.all_gather(query, ("tensor", "kv"), axis=1, tiled=True)
    grouped = queries.reshape(seqs, KVH, group, HD)
    span = kv_cache.shape[2]
    places = mine * span + jnp.arange(span, dtype=jnp.int32)
    live = (places[None, :] < lengths[:, None])[:, None, None, :]
    scores = (
        jnp.einsum("bgjd,bpgd->bgjp", grouped, kv_cache[0], preferred_element_type=jnp.float32)
        * scaling
    )
    scores = jnp.where(live, scores, floor_value)
    highest = jnp.max(scores, axis=3)
    weights = jnp.where(live, jnp.exp(scores - highest[..., None]), 0.0)
    totals = jnp.sum(weights, axis=3)
    accum = jnp.einsum("bgjp,bpgd->bgjd", weights, kv_cache[1], preferred_element_type=jnp.float32)
    highest = highest.reshape(seqs, QH)
    totals = totals.reshape(seqs, QH)
    accum = accum.reshape(seqs, QH, HD)
    arrived = (
        lax.all_to_all(highest[None], ("tensor", "kv"), split_axis=2, concat_axis=0, tiled=True),
        lax.all_to_all(totals[None], ("tensor", "kv"), split_axis=2, concat_axis=0, tiled=True),
        lax.all_to_all(accum[None], ("tensor", "kv"), split_axis=2, concat_axis=0, tiled=True),
    )
    best = jnp.max(arrived[0], axis=0)
    factor = jnp.exp(arrived[0] - best[None])
    totals = jnp.sum(arrived[1] * factor, axis=0)
    accum = jnp.sum(arrived[2] * factor[..., None], axis=0)
    highest = best
    own_query = query.reshape(seqs, per_dev, HD).astype(jnp.float32)
    head_ids = mine * per_dev + jnp.arange(per_dev, dtype=jnp.int32)
    selector = (head_ids[:, None] // group == jnp.arange(KVH, dtype=jnp.int32)[None, :]).astype(
        jnp.float32
    )
    fresh_pair = jnp.einsum("hg,sbgd->sbhd", selector, new_pair.astype(jnp.float32))
    fresh = jnp.sum(own_query * fresh_pair[0], axis=2) * scaling
    best = jnp.maximum(highest, fresh)
    old_factor = jnp.exp(highest - best)
    new_factor = jnp.exp(fresh - best)
    totals = totals * old_factor + new_factor
    accum = accum * old_factor[..., None] + new_factor[..., None] * fresh_pair[1]
    attended = (accum / totals[..., None]).astype(jnp.bfloat16).reshape(seqs, per_dev * HD)
    partial_value = jnp.dot(attended, out_weight, preferred_element_type=jnp.float32)
    gain_wide = norm_gain.astype(jnp.float32)
    share = lax.psum_scatter(partial_value, ("tensor", "kv"), scatter_dimension=1, tiled=True)
    stream = (residual.astype(jnp.float32) + share).astype(jnp.bfloat16)
    widened = stream.astype(jnp.float32)
    squares = lax.psum(jnp.sum(widened * widened, axis=1), ("tensor", "kv"))
    gain_mine = lax.dynamic_slice_in_dim(gain_wide, mine * width, width, 0)
    piece = (widened * lax.rsqrt(squares / D + epsilon)[:, None] * gain_mine[None, :]).astype(
        jnp.bfloat16
    )
    normed = lax.all_gather(piece, ("tensor", "kv"), axis=1, tiled=True)
    return (stream, normed)


def solution(mesh):
    placed = (
        P(("groups", "dp"), ("tensor", "kv")),
        P(("groups", "dp"), ("tensor", "kv")),
        P(None, ("groups", "dp"), None, None),
        P(None, ("groups", "dp"), ("tensor", "kv"), None, None),
        P(("groups", "dp")),
        P(("tensor", "kv"), None),
        P(),
    )
    return jax.shard_map(
        on_device,
        mesh=mesh,
        in_specs=placed,
        out_specs=(P(("groups", "dp"), ("tensor", "kv")), P(("groups", "dp"), None)),
        check_vma=False,
    )
```

profile of v0, /device:TPU:0, one launch (start us, length us, event | category | flops | bytes accessed | tf_op | source)
XLA Modules:
  0.0 155.4 jit_solution(17761867516999163748)
XLA Ops:
  7.2 0.0 copy-start
  7.2 0.0 copy-start.2
  7.2 0.0 copy-start.4
  7.2 7.0 %fusion.25 = (bf16[1,16,256,4,128]{4,3,2,1,0:T(4,128)(2,1)}, bf16[1,16,256,4,128]{4,3,2,1,0:T(4,128)(2,1)S(1)}) fusion(bf16[2,16,256,4,128]{4,3,2,1,0:T(4,128)(2,1)} %param.10), kind=kLoop, calls=%fused_computation.48 | loop fusion | bytes 16777216 | tf_op jit(solution)/shard_map/slice | solution.py:35
  14.2 0.0 copy-done.2
  14.2 15.9 %all_gather.6 = bf16[16,8192]{1,0:T(8,128)(2,1)S(1)} all-gather(bf16[16,1024]{1,0:T(8,128)(2,1)S(1)} %copy-done.2), channel_id=1, replica_groups=mesh['groups'=2,'tensor'=4,'dp'=2,'kv'=2] {'tensor','kv'}, dimensions={1}, use_global_device_ids=true | all-gather | bytes 294912 | tf_op jit(solution)/shard_map/all_gather | solution.py:22
  30.2 0.1 broadcast_compare_fusion
  30.3 1.3 fusion.26
  31.6 0.4 fusion.4
  32.0 0.1 copy.42
  32.1 0.6 broadcast.100
  32.6 0.7 reduce.1
  33.3 0.7 reshape.118
  34.0 4.7 %all-to-all-start.2 = ((f32[8,1,128]{2,1,0:T(1,128)}), f32[8,1,128]{2,1,0:T(1,128)S(1)}, u32[]{:S(2)}, u32[]{:S(2)}) async-start(f32[8,1,128]{2,1,0:T(1,128)} %reshape.118), calls=%async_computation.2 | async-start | bytes 8192 | tf_op jit(solution)/shard_map/all_to_all | solution.py:41
  38.7 0.1 copy.35
  38.8 0.7 reduce.3
  39.5 0.7 reshape.116
  40.2 4.1 %all-to-all-done.2 = f32[8,1,128]{2,1,0:T(1,128)S(1)} async-done(((f32[8,1,128]{2,1,0:T(1,128)}), f32[8,1,128]{2,1,0:T(1,128)S(1)}, u32[]{:S(2)}, u32[]{:S(2)}) %all-to-all-start.2) | async-done | bytes 4128 | tf_op jit(solution)/shard_map/all_to_all | solution.py:41
  44.2 3.3 %all-to-all-start.1 = ((f32[8,1,128]{2,1,0:T(1,128)}), f32[8,1,128]{2,1,0:T(1,128)S(1)}, u32[]{:S(2)}, u32[]{:S(2)}) async-start(f32[8,1,128]{2,1,0:T(1,128)} %reshape.116), calls=%async_computation.1 | async-start | bytes 8192 | tf_op jit(solution)/shard_map/all_to_all | solution.py:40
  47.5 2.9 %fusion = f32[16,4,16,128]{3,2,1,0:T(8,128)S(1)} fusion(bf16[1,16,256,4,128]{4,3,2,1,0:T(4,128)(2,1)} %get-tuple-element.9, f32[16,4,16,256]{3,2,1,0:T(8,128)S(1)} %get-tuple-element.12, f32[16,4,16]{2,1,0:T(4,128)S(1)} %get-tuple-element.11, pred[16,256]{1,0:T(8,128)(4,1)S(1)} %broadcast_compare_fusion), kind=kOutput, calls=%fused_computation.1 | convolution fusion | flops 67633152 | bytes 5775360 | tf_op jit(solution)/shard_map/bgjp,bpgd->bgjd/dot_general | solution.py:35
  50.4 1.1 copy.34
  51.5 1.5 all-to-all-done.1
  53.0 3.5 %all-to-all-start = ((f32[1,16,64,128]{3,1,0,2:T(8,128)}), f32[1,16,64,128]{3,1,0,2:T(8,128)S(1)}, u32[]{:S(2)}, u32[]{:S(2)}) async-start(f32[1,16,64,128]{3,1,0,2:T(8,128)} %copy.34), calls=%async_computation | async-start | bytes 1048576 | tf_op jit(solution)/shard_map/all_to_all | solution.py:42
  56.5 0.0 reduce-scatter.2.cloned.1.call-start
  56.6 0.2 convolution_bitcast_fusion
  56.9 0.1 fusion.14
  57.0 0.1 copy.36
  57.0 0.6 reduce.2
  57.7 0.1 reshape.119
  57.8 0.6 reduce.4
  58.4 0.1 reshape.117
  58.6 0.1 copy.38
  58.6 0.1 copy.40
  58.7 13.1 %all-to-all-done = f32[1,16,64,128]{3,1,0,2:T(8,128)S(1)} async-done(((f32[1,16,64,128]{3,1,0,2:T(8,128)}), f32[1,16,64,128]{3,1,0,2:T(8,128)S(1)}, u32[]{:S(2)}, u32[]{:S(2)}) %all-to-all-start) | async-done | bytes 524320 | tf_op jit(solution)/shard_map/all_to_all | solution.py:42
  71.9 0.2 multiply_reduce_fusion
  72.1 0.1 mul.110
  72.1 0.1 div.30
  72.2 0.0 copy-start.3
  72.2 13.9 %fusion.15 = f32[16,16384]{1,0:T(8,128)} fusion(bf16[1024,16384]{1,0:T(8,128)(2,1)} %param.12, f32[2,8,8,128]{3,2,1,0:T(8,128)S(1)} %bitcast.90, f32[2,8,8,128]{3,2,1,0:T(8,128)S(1)} %bitcast.88, f32[2,8,8,128]{3,2,1,0:T(8,128)S(1)} %bitcast.89, f32[16,8,128]{2,0,1:T(8,128)S(1)} %multiply_reduce_fusion, f32[16,8]{0,1:T(8,128)S(1)} %get-tuple-element.5), kind=kOutput, calls=%fused_computation.28 | convolution fusion | flops 536952832 | bytes 34865664 | tf_op jit(solution)/shard_map/dot_general | solution.py:62
  86.2 0.0 reduce-scatter.2.cloned.1.call-update
  86.2 0.7 dynamic-slice_convert_fusion
  86.9 31.0 %reduce-scatter.2.cloned.1.call-done = f32[16,2048]{1,0:T(8,128)} async-done(((f32[16,16384]{1,0:T(8,128)}), f32[16,2048]{1,0:T(8,128)}) %reduce-scatter.2.cloned.1.call-update) | async-done | bytes 131088 | tf_op jit(solution)/shard_map/reduce_scatter | solution.py:64
  117.9 1.0 fusion.8
  118.9 13.8 %psum.7 = f32[16]{0:T(128)S(1)} all-reduce(f32[16]{0:T(128)S(1)} %get-tuple-element.2), channel_id=1, replica_groups=mesh['groups'=2,'tensor'=4,'dp'=2,'kv'=2] {'tensor','kv'}, use_global_device_ids=true, to_apply=%region_8.9 | all-reduce | flops 16 | bytes 128 | tf_op jit(solution)/shard_map/psum | solution.py:67
  132.8 0.1 fusion.10
  132.9 14.9 %all_gather.7 = bf16[16,16384]{1,0:T(8,128)(2,1)S(1)} all-gather(bf16[16,2048]{1,0:T(8,128)(2,1)S(1)} %fusion.10), channel_id=1, replica_groups=mesh['groups'=2,'tensor'=4,'dp'=2,'kv'=2] {'tensor','kv'}, dimensions={1}, use_global_device_ids=true | all-gather | bytes 589824 | tf_op jit(solution)/shard_map/all_gather | solution.py:72
  147.8 0.8 copy.70
  148.6 0.0 copy-done.1
  (14 shorter events, 0.1 us)
Async XLA Ops:
  7.2 49.5 %copy-start = (bf16[2,16,4,128]{3,2,1,0:T(4,128)(2,1)S(1)}, bf16[2,16,4,128]{3,2,1,0:T(4,128)(2,1)}, u32[]{:S(2)}) copy-start(bf16[2,16,4,128]{3,2,1,0:T(4,128)(2,1)} %param.9) | copy-start | bytes 98308
  7.2 7.0 %copy-start.2 = (bf16[16,1024]{1,0:T(8,128)(2,1)S(1)}, bf16[16,1024]{1,0:T(8,128)(2,1)}, u32[]{:S(2)}) copy-start(bf16[16,1024]{1,0:T(8,128)(2,1)} %param.8) | copy-start | bytes 98308
  7.2 23.0 %copy-start.4 = (s32[16]{0:T(128)S(1)}, s32[16]{0:T(128)}, u32[]{:S(2)}) copy-start(s32[16]{0:T(128)} %param.11) | copy-start | bytes 196
  34.0 10.2 %all-to-all-start.2 = ((f32[8,1,128]{2,1,0:T(1,128)}), f32[8,1,128]{2,1,0:T(1,128)S(1)}, u32[]{:S(2)}, u32[]{:S(2)}) async-start(f32[8,1,128]{2,1,0:T(1,128)} %reshape.118), calls=%async_computation.2 | async-start | bytes 8192 | tf_op jit(solution)/shard_map/all_to_all | solution.py:41
  44.2 8.8 %all-to-all-start.1 = ((f32[8,1,128]{2,1,0:T(1,128)}), f32[8,1,128]{2,1,0:T(1,128)S(1)}, u32[]{:S(2)}, u32[]{:S(2)}) async-start(f32[8,1,128]{2,1,0:T(1,128)} %reshape.116), calls=%async_computation.1 | async-start | bytes 8192 | tf_op jit(solution)/shard_map/all_to_all | solution.py:40
  53.0 18.9 %all-to-all-start = ((f32[1,16,64,128]{3,1,0,2:T(8,128)}), f32[1,16,64,128]{3,1,0,2:T(8,128)S(1)}, u32[]{:S(2)}, u32[]{:S(2)}) async-start(f32[1,16,64,128]{3,1,0,2:T(8,128)} %copy.34), calls=%async_computation | async-start | bytes 1048576 | tf_op jit(solution)/shard_map/all_to_all | solution.py:42
  56.5 61.3 %reduce-scatter.2.cloned.1.call-start = ((), (), s32[]{:S(2)}) async-start(), calls=%async_computation.4 | async-start | bytes 1179648 | tf_op jit(solution)/shard_map/reduce_scatter | solution.py:64
  72.2 45.7 %copy-start.3 = (bf16[16,2048]{1,0:T(8,128)(2,1)S(1)}, bf16[16,2048]{1,0:T(8,128)(2,1)}, u32[]{:S(2)}) copy-start(bf16[16,2048]{1,0:T(8,128)(2,1)} %param.7) | copy-start | bytes 196612
  118.9 29.7 %copy-start.1 = (bf16[16,2048]{1,0:T(8,128)(2,1)}, bf16[16,2048]{1,0:T(8,128)(2,1)S(1)}, u32[]{:S(2)}) copy-start(bf16[16,2048]{1,0:T(8,128)(2,1)S(1)} %get-tuple-element.15) | copy-start | bytes 196612
Sparse Core Ops, SparseCore 0:
  86.3 31.5 reduce-scatter.1
where the time goes:
time: 156 us; the launch traced here: 155 us
  waiting for transfers between devices  49.7 us (32%)
  blocking collectives  44.7 us (29%)
  matrix products  18.3 us (12%)
  between operations  14.2 us (9%)
  local copies, waits for them, and re-layouts  11.7 us (8%)
  starting transfers between devices  11.5 us (7%)
  other arithmetic  5.32 us (3%)
    reduce_scatter x1, waiting for transfers between devices, on_device(): lax.psum_scatter(partial_value, ('tensor', 'kv'), scatter_dimension=1, ti...  31 us
    all_gather x1, blocking collectives, on_device(): queries = lax.all_gather(query, ('tensor', 'kv'), axis=1, tiled=True)  15.9 us
    all_gather x1, blocking collectives, on_device(): normed = lax.all_gather(piece, ('tensor', 'kv'), axis=1, tiled=True)  14.9 us
    dot_general x1, matrix products, on_device(): jnp.dot(attended, out_weight, preferred_element_type=jnp.float32)  13.9 us
    psum x1, blocking collectives, on_device(): squares = lax.psum(jnp.sum(widened * widened, axis=1), ('tensor', 'kv'))  13.8 us
    all_to_all x1, waiting for transfers between devices, on_device(): lax.all_to_all(accum[None], ('tensor', 'kv'), split_axis=2, concat_axis=0...  13.1 us
    slice x1, local copies, waits for them, and re-layouts, on_device(): kv_cache[1]  7.01 us
    all_to_all x1, starting transfers between devices, on_device(): lax.all_to_all(totals[None], ('tensor', 'kv'), split_axis=2, concat_axis=...  4.68 us
  transfers between devices with their start and end apart: 4, of which 4 were waited for; matrix products, arithmetic and copies ran while one was open for 5% of the time, Pallas kernels for 0%

commit v1 on v0

--- a/solution.py
+++ b/solution.py
@@ -39,7 +39,15 @@
     arrived = (
         lax.all_to_all(highest[None], ("tensor", "kv"), split_axis=2, concat_axis=0, tiled=True),
         lax.all_to_all(totals[None], ("tensor", "kv"), split_axis=2, concat_axis=0, tiled=True),
-        lax.all_to_all(accum[None], ("tensor", "kv"), split_axis=2, concat_axis=0, tiled=True),
+        jnp.concatenate(
+            lax.all_to_all(
+                jnp.stack(jnp.split(accum[None], lax.axis_size(("tensor", "kv")), axis=2)),
+                ("tensor", "kv"),
+                0,
+                0,
+            ),
+            axis=0,
+        ),
     )
     best = jnp.max(arrived[0], axis=0)
     factor = jnp.exp(arrived[0] - best[None])

time: 156 us -> 161 us (1.032)
  local copies, waits for them, and re-layouts: 11.7 us -> 15.8 us
  starting transfers between devices: 11.5 us -> 13.3 us
    unnamed x18 -> x25, local copies, waits for them, and re-layouts: 3 us -> 7.46 us
    all_to_all x1, waiting for transfers between devices: 4.05 us -> 0.01 us  [on_device(): lax.all_to_all(totals[None], ('tensor', 'kv'), split_axis=2, concat_axis=...]
    all_to_all x1, waiting for transfers between devices: 1.5 us -> 4.94 us  [on_device(): lax.all_to_all(highest[None], ('tensor', 'kv'), split_axis=2, concat_axis...]
    all_to_all x1, starting transfers between devices: 3.26 us -> 5.1 us  [on_device(): lax.all_to_all(highest[None], ('tensor', 'kv'), split_axis=2, concat_axis...]
  transfers between devices with their start and end apart: 4 -> 4, of which waited for: 4 -> 3; matrix products, arithmetic and copies ran while one was open for 5% -> 8% of each run, Pallas kernels for 0% -> 0%
where the time goes in v1:
time: 161 us
  waiting for transfers between devices  48.8 us (30%)
  blocking collectives  44.7 us (28%)
  matrix products  18.3 us (11%)
  local copies, waits for them, and re-layouts  15.8 us (10%)
  between operations  14.3 us (9%)
  starting transfers between devices  13.3 us (8%)
  other arithmetic  5.44 us (3%)
    reduce_scatter x1, waiting for transfers between devices, on_device(): lax.psum_scatter(partial_value, ('tensor', 'kv'), scatter_dimension=1, ti...  31 us
    all_gather x1, blocking collectives, on_device(): queries = lax.all_gather(query, ('tensor', 'kv'), axis=1, tiled=True)  15.9 us
    all_gather x1, blocking collectives, on_device(): normed = lax.all_gather(piece, ('tensor', 'kv'), axis=1, tiled=True)  14.9 us
    dot_general x1, matrix products, on_device(): jnp.dot(attended, out_weight, preferred_element_type=jnp.float32)  13.9 us
    psum x1, blocking collectives, on_device(): squares = lax.psum(jnp.sum(widened * widened, axis=1), ('tensor', 'kv'))  13.8 us
    all_to_all x1, waiting for transfers between devices, on_device(): lax.all_to_all(jnp.stack(jnp.split(accum[None], lax.axis_size(('tensor',...  12.9 us
    unnamed x25, local copies, waits for them, and re-layouts  7.46 us
    slice x1, local copies, waits for them, and re-layouts, on_device(): kv_cache[1]  7.01 us
  transfers between devices with their start and end apart: 4, of which 3 were waited for; matrix products, arithmetic and copies ran while one was open for 8% of the time, Pallas kernels for 0%

profile of v1, /device:TPU:0, one launch (start us, length us, event | category | flops | bytes accessed | tf_op | source)
XLA Modules:
  0.0 160.6 jit_solution(4873312676708682732)
XLA Ops:
  7.2 7.0 %fusion.34 = (bf16[1,16,256,4,128]{4,3,2,1,0:T(4,128)(2,1)}, bf16[1,16,256,4,128]{4,3,2,1,0:T(4,128)(2,1)S(1)}) fusion(bf16[2,16,256,4,128]{4,3,2,1,0:T(4,128)(2,1)} %param.10), kind=kLoop, calls=%fused_computation.65 | loop fusion | bytes 16777216 | tf_op jit(solution)/shard_map/slice | solution.py:35
  14.2 15.9 %all_gather.6 = bf16[16,8192]{1,0:T(8,128)(2,1)S(1)} all-gather(bf16[16,1024]{1,0:T(8,128)(2,1)S(1)} %copy-done.2), channel_id=1, replica_groups=mesh['groups'=2,'tensor'=4,'dp'=2,'kv'=2] {'tensor','kv'}, dimensions={1}, use_global_device_ids=true | all-gather | bytes 294912 | tf_op jit(solution)/shard_map/all_gather | solution.py:22
  30.2 0.1 broadcast_compare_fusion
  30.3 1.3 fusion.35
  31.6 0.4 fusion.4
  32.0 0.1 copy.35
  32.1 0.5 broadcast.100
  32.6 0.7 reduce.1
  33.3 0.7 reshape.122
  34.0 4.7 %all-to-all-start.2 = ((f32[8,1,128]{2,1,0:T(1,128)}), f32[8,1,128]{2,1,0:T(1,128)S(1)}, u32[]{:S(2)}, u32[]{:S(2)}) async-start(f32[8,1,128]{2,1,0:T(1,128)} %reshape.122), calls=%async_computation.2 | async-start | bytes 8192 | tf_op jit(solution)/shard_map/all_to_all | solution.py:41
  38.7 2.9 %fusion = f32[16,4,16,128]{3,2,1,0:T(8,128)S(1)} fusion(bf16[1,16,256,4,128]{4,3,2,1,0:T(4,128)(2,1)} %get-tuple-element.9, f32[16,4,16,256]{3,2,1,0:T(8,128)S(1)} %get-tuple-element.12, f32[16,4,16]{2,1,0:T(4,128)S(1)} %get-tuple-element.11, pred[16,256]{1,0:T(8,128)(4,1)S(1)} %broadcast_compare_fusion), kind=kOutput, calls=%fused_computation.1 | convolution fusion | flops 67633152 | bytes 5775360 | tf_op jit(solution)/shard_map/bgjp,bpgd->bgjd/dot_general | solution.py:35
  41.6 0.7 fusion.23
  42.2 0.6 fusion.22
  42.9 0.6 fusion.21
  43.5 0.6 fusion.20
  44.2 0.6 fusion.19
  44.8 0.6 fusion.18
  45.4 0.6 fusion.17
  46.1 0.1 copy.27
  46.1 0.7 reduce.3
  46.9 0.7 reshape.120
  47.5 5.1 %all-to-all-start.1 = ((f32[8,1,128]{2,1,0:T(1,128)}), f32[8,1,128]{2,1,0:T(1,128)S(1)}, u32[]{:S(2)}, u32[]{:S(2)}) async-start(f32[8,1,128]{2,1,0:T(1,128)} %reshape.120), calls=%async_computation.1 | async-start | bytes 8192 | tf_op jit(solution)/shard_map/all_to_all | solution.py:40
  52.6 0.6 fusion.16
  53.3 4.9 %all-to-all-done.1 = f32[8,1,128]{2,1,0:T(1,128)S(1)} async-done(((f32[8,1,128]{2,1,0:T(1,128)}), f32[8,1,128]{2,1,0:T(1,128)S(1)}, u32[]{:S(2)}, u32[]{:S(2)}) %all-to-all-start.1) | async-done | bytes 4128 | tf_op jit(solution)/shard_map/all_to_all | solution.py:40
  58.2 3.5 %all-to-all-start = ((f32[8,1,16,8,128]{4,3,2,1,0:T(8,128)}), f32[8,1,16,8,128]{4,3,2,1,0:T(8,128)S(1)}, u32[]{:S(2)}, u32[]{:S(2)}) async-start(f32[8,1,16,8,128]{4,3,2,1,0:T(8,128)} %fusion.16), calls=%async_computation | async-start | bytes 1048576 | tf_op jit(solution)/shard_map/all_to_all | solution.py:43
  61.8 0.2 convolution_bitcast_fusion
  62.1 0.1 fusion.15
  62.2 0.6 reduce.2
  62.9 0.1 reshape.123
  63.0 0.6 reduce.4
  63.6 0.1 reshape.121
  63.8 0.1 copy.28
  63.9 0.1 copy.30
  63.9 0.1 copy.31
  64.0 0.1 copy.33
  64.1 12.9 %all-to-all-done = f32[8,1,16,8,128]{4,3,2,1,0:T(8,128)S(1)} async-done(((f32[8,1,16,8,128]{4,3,2,1,0:T(8,128)}), f32[8,1,16,8,128]{4,3,2,1,0:T(8,128)S(1)}, u32[]{:S(2)}, u32[]{:S(2)}) %all-to-all-start) | async-done | bytes 524320 | tf_op jit(solution)/shard_map/all_to_all | solution.py:43
  77.0 0.2 fusion.5
  77.2 0.1 broadcast_multiply_fusion
  77.3 0.1 mul.110
  77.3 0.1 div.30
  77.4 13.9 %fusion.24 = f32[16,16384]{1,0:T(8,128)} fusion(bf16[1024,16384]{1,0:T(8,128)(2,1)} %param.12, f32[2,8,8,128]{3,2,1,0:T(8,128)S(1)} %bitcast.125, f32[2,8,8,128]{3,2,1,0:T(8,128)S(1)} %bitcast.122, f32[2,8,8,128]{3,2,1,0:T(8,128)S(1)} %bitcast.124, f32[2,8,8,128]{3,2,1,0:T(8,128)S(1)} %bitcast.123), kind=kOutput, calls=%fused_computation.44 | convolution fusion | flops 536936448 | bytes 34865152 | tf_op jit(solution)/shard_map/dot_general | solution.py:70
  91.4 0.7 dynamic-slice_convert_fusion
  92.1 31.0 %reduce-scatter.2.cloned.1.call-done = f32[16,2048]{1,0:T(8,128)} async-done(((f32[16,16384]{1,0:T(8,128)}), f32[16,2048]{1,0:T(8,128)}) %reduce-scatter.2.cloned.1.call-update) | async-done | bytes 131088 | tf_op jit(solution)/shard_map/reduce_scatter | solution.py:72
  123.0 1.0 fusion.9
  124.1 13.8 %psum.7 = f32[16]{0:T(128)S(1)} all-reduce(f32[16]{0:T(128)S(1)} %get-tuple-element.2), channel_id=1, replica_groups=mesh['groups'=2,'tensor'=4,'dp'=2,'kv'=2] {'tensor','kv'}, use_global_device_ids=true, to_apply=%region_8.9 | all-reduce | flops 16 | bytes 128 | tf_op jit(solution)/shard_map/psum | solution.py:75
  137.9 0.1 fusion.11
  138.0 14.9 %all_gather.7 = bf16[16,16384]{1,0:T(8,128)(2,1)S(1)} all-gather(bf16[16,2048]{1,0:T(8,128)(2,1)S(1)} %fusion.11), channel_id=1, replica_groups=mesh['groups'=2,'tensor'=4,'dp'=2,'kv'=2] {'tensor','kv'}, dimensions={1}, use_global_device_ids=true | all-gather | bytes 589824 | tf_op jit(solution)/shard_map/all_gather | solution.py:80
  152.9 0.8 copy.70
  (24 shorter events, 0.3 us)
Async XLA Ops:
  7.2 54.7 %copy-start = (bf16[2,16,4,128]{3,2,1,0:T(4,128)(2,1)S(1)}, bf16[2,16,4,128]{3,2,1,0:T(4,128)(2,1)}, u32[]{:S(2)}) copy-start(bf16[2,16,4,128]{3,2,1,0:T(4,128)(2,1)} %param.9) | copy-start | bytes 98308
  7.2 7.0 %copy-start.2 = (bf16[16,1024]{1,0:T(8,128)(2,1)S(1)}, bf16[16,1024]{1,0:T(8,128)(2,1)}, u32[]{:S(2)}) copy-start(bf16[16,1024]{1,0:T(8,128)(2,1)} %param.8) | copy-start | bytes 98308
  7.2 23.0 %copy-start.4 = (s32[16]{0:T(128)S(1)}, s32[16]{0:T(128)}, u32[]{:S(2)}) copy-start(s32[16]{0:T(128)} %param.11) | copy-start | bytes 196
  34.0 13.5 %all-to-all-start.2 = ((f32[8,1,128]{2,1,0:T(1,128)}), f32[8,1,128]{2,1,0:T(1,128)S(1)}, u32[]{:S(2)}, u32[]{:S(2)}) async-start(f32[8,1,128]{2,1,0:T(1,128)} %reshape.122), calls=%async_computation.2 | async-start | bytes 8192 | tf_op jit(solution)/shard_map/all_to_all | solution.py:41
  47.5 10.7 %all-to-all-start.1 = ((f32[8,1,128]{2,1,0:T(1,128)}), f32[8,1,128]{2,1,0:T(1,128)S(1)}, u32[]{:S(2)}, u32[]{:S(2)}) async-start(f32[8,1,128]{2,1,0:T(1,128)} %reshape.120), calls=%async_computation.1 | async-start | bytes 8192 | tf_op jit(solution)/shard_map/all_to_all | solution.py:40
  58.2 18.8 %all-to-all-start = ((f32[8,1,16,8,128]{4,3,2,1,0:T(8,128)}), f32[8,1,16,8,128]{4,3,2,1,0:T(8,128)S(1)}, u32[]{:S(2)}, u32[]{:S(2)}) async-start(f32[8,1,16,8,128]{4,3,2,1,0:T(8,128)} %fusion.16), calls=%async_computation | async-start | bytes 1048576 | tf_op jit(solution)/shard_map/all_to_all | solution.py:43
  61.7 61.3 %reduce-scatter.2.cloned.1.call-start = ((), (), s32[]{:S(2)}) async-start(), calls=%async_computation.4 | async-start | bytes 1179648 | tf_op jit(solution)/shard_map/reduce_scatter | solution.py:72
  77.4 45.6 %copy-start.3 = (bf16[16,2048]{1,0:T(8,128)(2,1)S(1)}, bf16[16,2048]{1,0:T(8,128)(2,1)}, u32[]{:S(2)}) copy-start(bf16[16,2048]{1,0:T(8,128)(2,1)} %param.7) | copy-start | bytes 196612
  124.1 29.7 %copy-start.1 = (bf16[16,2048]{1,0:T(8,128)(2,1)}, bf16[16,2048]{1,0:T(8,128)(2,1)S(1)}, u32[]{:S(2)}) copy-start(bf16[16,2048]{1,0:T(8,128)(2,1)S(1)} %get-tuple-element.15) | copy-start | bytes 196612
Sparse Core Ops, SparseCore 0:
  91.5 31.4 reduce-scatter.1
